TPU v7x, 32 devices: a whole 2x2x4 slice. The times are simulated.
32 devices in a mesh: blk: 16 (over z, y, core), rows: 2 (over x).
Axes of the slice: x: 2, y: 2, z: 4, core: 2. Of those that a mesh axis runs over, the one named last changes fastest.
Arguments:
- columns: float32 [2048, 1280], P('blk', 'rows'), may hold values from -9 to 9
- right_factor: float32 [2048, 512], P('blk', 'rows'), may hold values from -6 to 6
Outputs:
- new_columns: float32 [2048, 1280], P('blk', 'rows')
- new_factor: float32 [2048, 512], P('blk', 'rows')
All inputs are finite; a program needn't handle non-finite values.
Results may differ from a plain program's by a relative error of at most 0.0003.
Values sent between devices are 32-bit elements; how exact they have to be, the bound alone decides.
A program may use at most 64 MiB of HBM per device.

v0:
```python
import jax
import jax.numpy as jnp
from jax import lax
from jax.sharding import PartitionSpec as P

STEPS = 6
HIGHEST_PREC = lax.Precision.HIGHEST


def shifted(block, axis, distance):
    devices = range(lax.axis_size(axis))
    route = [((i - distance) % len(devices), i) for i in devices]
    return lax.ppermute(block, axis, route)


def orth_factor(square):
    lower_factor = jnp.linalg.cholesky(jnp.dot(square.T, square, precision=HIGHEST_PREC))
    return jax.scipy.linalg.solve_triangular(lower_factor, square.T, lower=True).T


def rotation(pair_gram):
    first_turn = orth_factor(pair_gram)
    return orth_factor(jnp.dot(pair_gram, first_turn, precision=HIGHEST_PREC))


def gram_of(upper_rows, lower_rows):
    return lax.dot_general(upper_rows, lower_rows, (((1,), (1,)), ((), ())), precision=HIGHEST_PREC)


def rotate(rotation_matrix, blocks):
    return lax.dot_general(
        rotation_matrix, blocks, (((0,), (0,)), ((), ())), precision=HIGHEST_PREC
    )


def body(columns, right_factor):
    block_width = columns.shape[0] // 2
    stay_gram, moving_gram = lax.psum(
        (
            gram_of(columns[:block_width], columns[:block_width]),
            gram_of(columns[block_width:], columns[block_width:]),
        ),
        "rows",
    )

    def advance_cross(step_index, loop_state):
        column_pair, factor_pair, stay_gram, moving_gram = loop_state
        cross_term = lax.psum(gram_of(column_pair[:block_width], column_pair[block_width:]), "rows")
        upper_half = jnp.concatenate([stay_gram, cross_term], 1)
        lower_half = jnp.concatenate([cross_term.T, moving_gram], 1)
        pair_gram = jnp.concatenate([upper_half, lower_half], 0)
        rotation_matrix = rotation(pair_gram)
        column_pair = rotate(rotation_matrix, column_pair)
        factor_pair = rotate(rotation_matrix, factor_pair)
        rotated_gram = rotate(
            rotation_matrix, jnp.dot(pair_gram, rotation_matrix, precision=HIGHEST_PREC)
        )
        arrived = shifted(
            (
                column_pair[block_width:],
                factor_pair[block_width:],
                rotated_gram[block_width:, block_width:],
            ),
            "blk",
            1,
        )
        return (
            jnp.concatenate([column_pair[:block_width], arrived[0]], 0),
            jnp.concatenate([factor_pair[:block_width], arrived[1]], 0),
            rotated_gram[:block_width, :block_width],
            arrived[2],
        )

    result = lax.fori_loop(0, STEPS, advance_cross, (columns, right_factor, stay_gram, moving_gram))
    return (result[0], result[1])


def solution(mesh):
    return jax.shard_map(
        body,
        mesh=mesh,
        in_specs=(P("blk", "rows"), P("blk", "rows")),
        out_specs=(P("blk", "rows"), P("blk", "rows")),
        check_vma=False,
    )
```

profile of v0, /device:TPU:0, one launch (start us, length us, event | category | flops | bytes accessed | tf_op | source)
XLA Modules:
  0.0 402.2 jit_solution(8088612820644958071)
XLA Ops:
  2.2 10.4 %all-reduce = (f32[64,64]{1,0:T(8,128)S(1)}, f32[64,64]{1,0:T(8,128)S(1)}) all-reduce(f32[64,64]{1,0:T(8,128)S(1)} %fusion.17, f32[64,64]{1,0:T(8,128)S(1)} %fusion.15), channel_id=1, replica_groups=mesh['blk'=16,'rows'=2] {'rows'}, use_global_device_ids=true, to_apply=%region_0.0 | all-reduce | flops 8192 | bytes 65536 | tf_op jit(solution)/shard_map/psum | solution.py:38
  12.7 388.7 %while.16 = (s32[]{:T(128)}, f32[128,640]{1,0:T(8,128)S(1)}, f32[128,256]{1,0:T(8,128)S(1)}, f32[64,64]{1,0:T(8,128)S(1)}, f32[64,64]{1,0:T(8,128)S(1)}, /*index=5*/s32[]{:T(128)}) while((s32[]{:T(128)}, f32[128,640]{1,0:T(8,128)S(1)}, f32[128,256]{1,0:T(8,128)S(1)}, f32[64,64]{1,0:T(8,128)S(1)}, f32[64,64]{1,0:T(8,128)S(1)}, ...), condition=%wide.region_6.9_spmd, body=%wide.region_2.8_spmd.sunk | while | flops 384241920 | bytes 6834369 | solution.py:74
  13.2 6.9 %psum.24 = f32[64,64]{1,0:T(8,128)S(1)} all-reduce(f32[64,64]{1,0:T(8,128)S(1)} %fusion.101), channel_id=1, replica_groups=mesh['blk'=16,'rows'=2] {'rows'}, use_global_device_ids=true, to_apply=%region_3.0 | all-reduce | flops 4096 | bytes 32768 | tf_op jit(solution)/shard_map/while/body/eval_jaxpr/psum | solution.py:48
  20.7 11.7 %cholesky.144 = f32[128,128]{1,0:T(8,128)S(1)} custom-call(f32[128,128]{1,0:T(8,128)S(1)} %fusion.103), custom_call_target="Cholesky" | custom-call | tf_op jit(solution)/shard_map/while/body/eval_jaxpr/jit(cholesky)/cholesky | solution.py:17
  33.7 9.8 %custom-call.10 = f32[1,128,128]{1,2,0:T(8,128)S(1)} custom-call(f32[1,128,128]{2,1,0:T(8,128)S(1)} %fusion.105), custom_call_target="InvertDiagBlocksLowerTriangular" | custom-call | tf_op jit(solution)/shard_map/while/body/eval_jaxpr/jit(_solve_triangular)/triangular_solve | solution.py:18
  44.5 11.7 %cholesky.145 = f32[128,128]{1,0:T(8,128)S(1)} custom-call(f32[128,128]{1,0:T(8,128)S(1)} %fusion.109), custom_call_target="Cholesky" | custom-call | tf_op jit(solution)/shard_map/while/body/eval_jaxpr/jit(cholesky)/cholesky | solution.py:17
  57.6 9.8 %custom-call.11 = f32[1,128,128]{1,2,0:T(8,128)S(1)} custom-call(f32[1,128,128]{2,1,0:T(8,128)S(1)} %fusion.110), custom_call_target="InvertDiagBlocksLowerTriangular" | custom-call | tf_op jit(solution)/shard_map/while/body/eval_jaxpr/jit(_solve_triangular)/triangular_solve | solution.py:18
  77.6 8.3 %psum.24 = f32[64,64]{1,0:T(8,128)S(1)} all-reduce(f32[64,64]{1,0:T(8,128)S(1)} %fusion.101), channel_id=1, replica_groups=mesh['blk'=16,'rows'=2] {'rows'}, use_global_device_ids=true, to_apply=%region_3.0 | all-reduce | flops 4096 | bytes 32768 | tf_op jit(solution)/shard_map/while/body/eval_jaxpr/psum | solution.py:48
  86.5 11.7 %cholesky.144 = f32[128,128]{1,0:T(8,128)S(1)} custom-call(f32[128,128]{1,0:T(8,128)S(1)} %fusion.103), custom_call_target="Cholesky" | custom-call | tf_op jit(solution)/shard_map/while/body/eval_jaxpr/jit(cholesky)/cholesky | solution.py:17
  99.5 9.8 %custom-call.10 = f32[1,128,128]{1,2,0:T(8,128)S(1)} custom-call(f32[1,128,128]{2,1,0:T(8,128)S(1)} %fusion.105), custom_call_target="InvertDiagBlocksLowerTriangular" | custom-call | tf_op jit(solution)/shard_map/while/body/eval_jaxpr/jit(_solve_triangular)/triangular_solve | solution.py:18
  110.4 11.7 %cholesky.145 = f32[128,128]{1,0:T(8,128)S(1)} custom-call(f32[128,128]{1,0:T(8,128)S(1)} %fusion.109), custom_call_target="Cholesky" | custom-call | tf_op jit(solution)/shard_map/while/body/eval_jaxpr/jit(cholesky)/cholesky | solution.py:17
  123.4 9.8 %custom-call.11 = f32[1,128,128]{1,2,0:T(8,128)S(1)} custom-call(f32[1,128,128]{2,1,0:T(8,128)S(1)} %fusion.110), custom_call_target="InvertDiagBlocksLowerTriangular" | custom-call | tf_op jit(solution)/shard_map/while/body/eval_jaxpr/jit(_solve_triangular)/triangular_solve | solution.py:18
  142.8 7.4 %psum.24 = f32[64,64]{1,0:T(8,128)S(1)} all-reduce(f32[64,64]{1,0:T(8,128)S(1)} %fusion.101), channel_id=1, replica_groups=mesh['blk'=16,'rows'=2] {'rows'}, use_global_device_ids=true, to_apply=%region_3.0 | all-reduce | flops 4096 | bytes 32768 | tf_op jit(solution)/shard_map/while/body/eval_jaxpr/psum | solution.py:48
  150.8 11.7 %cholesky.144 = f32[128,128]{1,0:T(8,128)S(1)} custom-call(f32[128,128]{1,0:T(8,128)S(1)} %fusion.103), custom_call_target="Cholesky" | custom-call | tf_op jit(solution)/shard_map/while/body/eval_jaxpr/jit(cholesky)/cholesky | solution.py:17
  163.8 9.8 %custom-call.10 = f32[1,128,128]{1,2,0:T(8,128)S(1)} custom-call(f32[1,128,128]{2,1,0:T(8,128)S(1)} %fusion.105), custom_call_target="InvertDiagBlocksLowerTriangular" | custom-call | tf_op jit(solution)/shard_map/while/body/eval_jaxpr/jit(_solve_triangular)/triangular_solve | solution.py:18
  174.6 11.7 %cholesky.145 = f32[128,128]{1,0:T(8,128)S(1)} custom-call(f32[128,128]{1,0:T(8,128)S(1)} %fusion.109), custom_call_target="Cholesky" | custom-call | tf_op jit(solution)/shard_map/while/body/eval_jaxpr/jit(cholesky)/cholesky | solution.py:17
  187.7 9.8 %custom-call.11 = f32[1,128,128]{1,2,0:T(8,128)S(1)} custom-call(f32[1,128,128]{2,1,0:T(8,128)S(1)} %fusion.110), custom_call_target="InvertDiagBlocksLowerTriangular" | custom-call | tf_op jit(solution)/shard_map/while/body/eval_jaxpr/jit(_solve_triangular)/triangular_solve | solution.py:18
  207.1 8.3 %psum.24 = f32[64,64]{1,0:T(8,128)S(1)} all-reduce(f32[64,64]{1,0:T(8,128)S(1)} %fusion.101), channel_id=1, replica_groups=mesh['blk'=16,'rows'=2] {'rows'}, use_global_device_ids=true, to_apply=%region_3.0 | all-reduce | flops 4096 | bytes 32768 | tf_op jit(solution)/shard_map/while/body/eval_jaxpr/psum | solution.py:48
  216.0 11.7 %cholesky.144 = f32[128,128]{1,0:T(8,128)S(1)} custom-call(f32[128,128]{1,0:T(8,128)S(1)} %fusion.103), custom_call_target="Cholesky" | custom-call | tf_op jit(solution)/shard_map/while/body/eval_jaxpr/jit(cholesky)/cholesky | solution.py:17
  229.1 9.8 %custom-call.10 = f32[1,128,128]{1,2,0:T(8,128)S(1)} custom-call(f32[1,128,128]{2,1,0:T(8,128)S(1)} %fusion.105), custom_call_target="InvertDiagBlocksLowerTriangular" | custom-call | tf_op jit(solution)/shard_map/while/body/eval_jaxpr/jit(_solve_triangular)/triangular_solve | solution.py:18
  239.9 11.7 %cholesky.145 = f32[128,128]{1,0:T(8,128)S(1)} custom-call(f32[128,128]{1,0:T(8,128)S(1)} %fusion.109), custom_call_target="Cholesky" | custom-call | tf_op jit(solution)/shard_map/while/body/eval_jaxpr/jit(cholesky)/cholesky | solution.py:17
  252.9 9.8 %custom-call.11 = f32[1,128,128]{1,2,0:T(8,128)S(1)} custom-call(f32[1,128,128]{2,1,0:T(8,128)S(1)} %fusion.110), custom_call_target="InvertDiagBlocksLowerTriangular" | custom-call | tf_op jit(solution)/shard_map/while/body/eval_jaxpr/jit(_solve_triangular)/triangular_solve | solution.py:18
  272.3 7.4 %psum.24 = f32[64,64]{1,0:T(8,128)S(1)} all-reduce(f32[64,64]{1,0:T(8,128)S(1)} %fusion.101), channel_id=1, replica_groups=mesh['blk'=16,'rows'=2] {'rows'}, use_global_device_ids=true, to_apply=%region_3.0 | all-reduce | flops 4096 | bytes 32768 | tf_op jit(solution)/shard_map/while/body/eval_jaxpr/psum | solution.py:48
  280.3 11.7 %cholesky.144 = f32[128,128]{1,0:T(8,128)S(1)} custom-call(f32[128,128]{1,0:T(8,128)S(1)} %fusion.103), custom_call_target="Cholesky" | custom-call | tf_op jit(solution)/shard_map/while/body/eval_jaxpr/jit(cholesky)/cholesky | solution.py:17
  293.4 9.8 %custom-call.10 = f32[1,128,128]{1,2,0:T(8,128)S(1)} custom-call(f32[1,128,128]{2,1,0:T(8,128)S(1)} %fusion.105), custom_call_target="InvertDiagBlocksLowerTriangular" | custom-call | tf_op jit(solution)/shard_map/while/body/eval_jaxpr/jit(_solve_triangular)/triangular_solve | solution.py:18
  304.2 11.7 %cholesky.145 = f32[128,128]{1,0:T(8,128)S(1)} custom-call(f32[128,128]{1,0:T(8,128)S(1)} %fusion.109), custom_call_target="Cholesky" | custom-call | tf_op jit(solution)/shard_map/while/body/eval_jaxpr/jit(cholesky)/cholesky | solution.py:17
  317.2 9.8 %custom-call.11 = f32[1,128,128]{1,2,0:T(8,128)S(1)} custom-call(f32[1,128,128]{2,1,0:T(8,128)S(1)} %fusion.110), custom_call_target="InvertDiagBlocksLowerTriangular" | custom-call | tf_op jit(solution)/shard_map/while/body/eval_jaxpr/jit(_solve_triangular)/triangular_solve | solution.py:18
  336.6 8.3 %psum.24 = f32[64,64]{1,0:T(8,128)S(1)} all-reduce(f32[64,64]{1,0:T(8,128)S(1)} %fusion.101), channel_id=1, replica_groups=mesh['blk'=16,'rows'=2] {'rows'}, use_global_device_ids=true, to_apply=%region_3.0 | all-reduce | flops 4096 | bytes 32768 | tf_op jit(solution)/shard_map/while/body/eval_jaxpr/psum | solution.py:48
  345.5 11.7 %cholesky.144 = f32[128,128]{1,0:T(8,128)S(1)} custom-call(f32[128,128]{1,0:T(8,128)S(1)} %fusion.103), custom_call_target="Cholesky" | custom-call | tf_op jit(solution)/shard_map/while/body/eval_jaxpr/jit(cholesky)/cholesky | solution.py:17
  358.6 9.8 %custom-call.10 = f32[1,128,128]{1,2,0:T(8,128)S(1)} custom-call(f32[1,128,128]{2,1,0:T(8,128)S(1)} %fusion.105), custom_call_target="InvertDiagBlocksLowerTriangular" | custom-call | tf_op jit(solution)/shard_map/while/body/eval_jaxpr/jit(_solve_triangular)/triangular_solve | solution.py:18
  369.4 11.7 %cholesky.145 = f32[128,128]{1,0:T(8,128)S(1)} custom-call(f32[128,128]{1,0:T(8,128)S(1)} %fusion.109), custom_call_target="Cholesky" | custom-call | tf_op jit(solution)/shard_map/while/body/eval_jaxpr/jit(cholesky)/cholesky | solution.py:17
  382.5 9.8 %custom-call.11 = f32[1,128,128]{1,2,0:T(8,128)S(1)} custom-call(f32[1,128,128]{2,1,0:T(8,128)S(1)} %fusion.110), custom_call_target="InvertDiagBlocksLowerTriangular" | custom-call | tf_op jit(solution)/shard_map/while/body/eval_jaxpr/jit(_solve_triangular)/triangular_solve | solution.py:18
  (219 shorter events, 85.0 us)
Async XLA Ops:
  1.9 10.8 %copy-start.2 = (f32[128,256]{1,0:T(8,128)S(1)}, f32[128,256]{1,0:T(8,128)}, u32[]{:S(2)}) copy-start(f32[128,256]{1,0:T(8,128)} %param.8) | copy-start | bytes 393220
  68.0 6.4 %collective-permute-start.1 = (f32[64,256]{1,0:T(8,128)S(1)}, f32[64,256]{1,0:T(8,128)S(1)}, u32[]{:S(2)}, u32[]{:S(2)}) collective-permute-start(f32[64,256]{1,0:T(8,128)S(1)} %get-tuple-element.91), channel_id=1, source_target_pairs={{30,0},{0,2},{2,4},{4,6},{6,8},{8,10},{10,12},{12,14},{14,16},{16,... | collective-permute-start | bytes 196616 | tf_op jit(solution)/shard_map/while/body/eval_jaxpr/ppermute | solution.py:13
  68.5 7.7 %collective-permute-start = (f32[64,640]{1,0:T(8,128)S(1)}, f32[64,640]{1,0:T(8,128)S(1)}, u32[]{:S(2)}, u32[]{:S(2)}) collective-permute-start(f32[64,640]{1,0:T(8,128)S(1)} %get-tuple-element.89), channel_id=1, source_target_pairs={{30,0},{0,2},{2,4},{4,6},{6,8},{8,10},{10,12},{12,14},{14,16},{16,... | collective-permute-start | bytes 491528 | tf_op jit(solution)/shard_map/while/body/eval_jaxpr/ppermute | solution.py:13
  71.1 6.0 %collective-permute-start.2 = (f32[64,64]{1,0:T(8,128)S(1)}, f32[64,64]{1,0:T(8,128)S(1)}, u32[]{:S(2)}, u32[]{:S(2)}) collective-permute-start(f32[64,64]{1,0:T(8,128)S(1)} %get-tuple-element.94), channel_id=1, source_target_pairs={{30,0},{0,2},{2,4},{4,6},{6,8},{8,10},{10,12},{12,14},{14,16},{16,... | collective-permute-start | bytes 49160 | tf_op jit(solution)/shard_map/while/body/eval_jaxpr/ppermute | solution.py:13
  133.8 6.4 %collective-permute-start.1 = (f32[64,256]{1,0:T(8,128)S(1)}, f32[64,256]{1,0:T(8,128)S(1)}, u32[]{:S(2)}, u32[]{:S(2)}) collective-permute-start(f32[64,256]{1,0:T(8,128)S(1)} %get-tuple-element.91), channel_id=1, source_target_pairs={{30,0},{0,2},{2,4},{4,6},{6,8},{8,10},{10,12},{12,14},{14,16},{16,... | collective-permute-start | bytes 196616 | tf_op jit(solution)/shard_map/while/body/eval_jaxpr/ppermute | solution.py:13
  134.3 7.7 %collective-permute-start = (f32[64,640]{1,0:T(8,128)S(1)}, f32[64,640]{1,0:T(8,128)S(1)}, u32[]{:S(2)}, u32[]{:S(2)}) collective-permute-start(f32[64,640]{1,0:T(8,128)S(1)} %get-tuple-element.89), channel_id=1, source_target_pairs={{30,0},{0,2},{2,4},{4,6},{6,8},{8,10},{10,12},{12,14},{14,16},{16,... | collective-permute-start | bytes 491528 | tf_op jit(solution)/shard_map/while/body/eval_jaxpr/ppermute | solution.py:13
  135.0 7.4 %collective-permute-start.2 = (f32[64,64]{1,0:T(8,128)S(1)}, f32[64,64]{1,0:T(8,128)S(1)}, u32[]{:S(2)}, u32[]{:S(2)}) collective-permute-start(f32[64,64]{1,0:T(8,128)S(1)} %get-tuple-element.94), channel_id=1, source_target_pairs={{30,0},{0,2},{2,4},{4,6},{6,8},{8,10},{10,12},{12,14},{14,16},{16,... | collective-permute-start | bytes 49160 | tf_op jit(solution)/shard_map/while/body/eval_jaxpr/ppermute | solution.py:13
  198.1 6.4 %collective-permute-start.1 = (f32[64,256]{1,0:T(8,128)S(1)}, f32[64,256]{1,0:T(8,128)S(1)}, u32[]{:S(2)}, u32[]{:S(2)}) collective-permute-start(f32[64,256]{1,0:T(8,128)S(1)} %get-tuple-element.91), channel_id=1, source_target_pairs={{30,0},{0,2},{2,4},{4,6},{6,8},{8,10},{10,12},{12,14},{14,16},{16,... | collective-permute-start | bytes 196616 | tf_op jit(solution)/shard_map/while/body/eval_jaxpr/ppermute | solution.py:13
  198.6 7.7 %collective-permute-start = (f32[64,640]{1,0:T(8,128)S(1)}, f32[64,640]{1,0:T(8,128)S(1)}, u32[]{:S(2)}, u32[]{:S(2)}) collective-permute-start(f32[64,640]{1,0:T(8,128)S(1)} %get-tuple-element.89), channel_id=1, source_target_pairs={{30,0},{0,2},{2,4},{4,6},{6,8},{8,10},{10,12},{12,14},{14,16},{16,... | collective-permute-start | bytes 491528 | tf_op jit(solution)/shard_map/while/body/eval_jaxpr/ppermute | solution.py:13
  199.2 7.4 %collective-permute-start.2 = (f32[64,64]{1,0:T(8,128)S(1)}, f32[64,64]{1,0:T(8,128)S(1)}, u32[]{:S(2)}, u32[]{:S(2)}) collective-permute-start(f32[64,64]{1,0:T(8,128)S(1)} %get-tuple-element.94), channel_id=1, source_target_pairs={{30,0},{0,2},{2,4},{4,6},{6,8},{8,10},{10,12},{12,14},{14,16},{16,... | collective-permute-start | bytes 49160 | tf_op jit(solution)/shard_map/while/body/eval_jaxpr/ppermute | solution.py:13
  263.3 6.4 %collective-permute-start.1 = (f32[64,256]{1,0:T(8,128)S(1)}, f32[64,256]{1,0:T(8,128)S(1)}, u32[]{:S(2)}, u32[]{:S(2)}) collective-permute-start(f32[64,256]{1,0:T(8,128)S(1)} %get-tuple-element.91), channel_id=1, source_target_pairs={{30,0},{0,2},{2,4},{4,6},{6,8},{8,10},{10,12},{12,14},{14,16},{16,... | collective-permute-start | bytes 196616 | tf_op jit(solution)/shard_map/while/body/eval_jaxpr/ppermute | solution.py:13
  263.8 7.7 %collective-permute-start = (f32[64,640]{1,0:T(8,128)S(1)}, f32[64,640]{1,0:T(8,128)S(1)}, u32[]{:S(2)}, u32[]{:S(2)}) collective-permute-start(f32[64,640]{1,0:T(8,128)S(1)} %get-tuple-element.89), channel_id=1, source_target_pairs={{30,0},{0,2},{2,4},{4,6},{6,8},{8,10},{10,12},{12,14},{14,16},{16,... | collective-permute-start | bytes 491528 | tf_op jit(solution)/shard_map/while/body/eval_jaxpr/ppermute | solution.py:13
  264.5 7.4 %collective-permute-start.2 = (f32[64,64]{1,0:T(8,128)S(1)}, f32[64,64]{1,0:T(8,128)S(1)}, u32[]{:S(2)}, u32[]{:S(2)}) collective-permute-start(f32[64,64]{1,0:T(8,128)S(1)} %get-tuple-element.94), channel_id=1, source_target_pairs={{30,0},{0,2},{2,4},{4,6},{6,8},{8,10},{10,12},{12,14},{14,16},{16,... | collective-permute-start | bytes 49160 | tf_op jit(solution)/shard_map/while/body/eval_jaxpr/ppermute | solution.py:13
  327.6 6.4 %collective-permute-start.1 = (f32[64,256]{1,0:T(8,128)S(1)}, f32[64,256]{1,0:T(8,128)S(1)}, u32[]{:S(2)}, u32[]{:S(2)}) collective-permute-start(f32[64,256]{1,0:T(8,128)S(1)} %get-tuple-element.91), channel_id=1, source_target_pairs={{30,0},{0,2},{2,4},{4,6},{6,8},{8,10},{10,12},{12,14},{14,16},{16,... | collective-permute-start | bytes 196616 | tf_op jit(solution)/shard_map/while/body/eval_jaxpr/ppermute | solution.py:13
  328.1 7.7 %collective-permute-start = (f32[64,640]{1,0:T(8,128)S(1)}, f32[64,640]{1,0:T(8,128)S(1)}, u32[]{:S(2)}, u32[]{:S(2)}) collective-permute-start(f32[64,640]{1,0:T(8,128)S(1)} %get-tuple-element.89), channel_id=1, source_target_pairs={{30,0},{0,2},{2,4},{4,6},{6,8},{8,10},{10,12},{12,14},{14,16},{16,... | collective-permute-start | bytes 491528 | tf_op jit(solution)/shard_map/while/body/eval_jaxpr/ppermute | solution.py:13
  328.8 7.4 %collective-permute-start.2 = (f32[64,64]{1,0:T(8,128)S(1)}, f32[64,64]{1,0:T(8,128)S(1)}, u32[]{:S(2)}, u32[]{:S(2)}) collective-permute-start(f32[64,64]{1,0:T(8,128)S(1)} %get-tuple-element.94), channel_id=1, source_target_pairs={{30,0},{0,2},{2,4},{4,6},{6,8},{8,10},{10,12},{12,14},{14,16},{16,... | collective-permute-start | bytes 49160 | tf_op jit(solution)/shard_map/while/body/eval_jaxpr/ppermute | solution.py:13
  392.8 6.4 %collective-permute-start.1 = (f32[64,256]{1,0:T(8,128)S(1)}, f32[64,256]{1,0:T(8,128)S(1)}, u32[]{:S(2)}, u32[]{:S(2)}) collective-permute-start(f32[64,256]{1,0:T(8,128)S(1)} %get-tuple-element.91), channel_id=1, source_target_pairs={{30,0},{0,2},{2,4},{4,6},{6,8},{8,10},{10,12},{12,14},{14,16},{16,... | collective-permute-start | bytes 196616 | tf_op jit(solution)/shard_map/while/body/eval_jaxpr/ppermute | solution.py:13
  393.4 7.7 %collective-permute-start = (f32[64,640]{1,0:T(8,128)S(1)}, f32[64,640]{1,0:T(8,128)S(1)}, u32[]{:S(2)}, u32[]{:S(2)}) collective-permute-start(f32[64,640]{1,0:T(8,128)S(1)} %get-tuple-element.89), channel_id=1, source_target_pairs={{30,0},{0,2},{2,4},{4,6},{6,8},{8,10},{10,12},{12,14},{14,16},{16,... | collective-permute-start | bytes 491528 | tf_op jit(solution)/shard_map/while/body/eval_jaxpr/ppermute | solution.py:13
  394.0 7.4 %collective-permute-start.2 = (f32[64,64]{1,0:T(8,128)S(1)}, f32[64,64]{1,0:T(8,128)S(1)}, u32[]{:S(2)}, u32[]{:S(2)}) collective-permute-start(f32[64,64]{1,0:T(8,128)S(1)} %get-tuple-element.94), channel_id=1, source_target_pairs={{30,0},{0,2},{2,4},{4,6},{6,8},{8,10},{10,12},{12,14},{14,16},{16,... | collective-permute-start | bytes 49160 | tf_op jit(solution)/shard_map/while/body/eval_jaxpr/ppermute | solution.py:13
  401.4 0.7 copy-start
  401.4 0.8 copy-start.1
where the time goes:
time: 403 us; the launch traced here: 402 us
  other arithmetic  275 us (68%)
  blocking collectives  57.1 us (14%)
  waiting for transfers between devices  42.6 us (11%)
  matrix products  17.9 us (4%)
  local copies, waits for them, and re-layouts  4.83 us (1%)
    another operation x36, other arithmetic, orth_factor(): jnp.linalg.cholesky(jnp.dot(square.T, square, precision=HIGHEST_PREC))  149 us
    another operation x24, other arithmetic, orth_factor(): jax.scipy.linalg.solve_triangular(lower_factor, square.T, lower=True)  126 us
    psum x6, blocking collectives, advance_cross(): lax.psum(gram_of(column_pair[:block_width], column_pair[block_width:]), '...  46.7 us
    ppermute x18, waiting for transfers between devices, shifted(): return lax.ppermute(block, axis, route)  42.6 us
    psum x1, blocking collectives, body(): lax.psum((gram_of(columns[:block_width], columns[:block_width]), gram_of(...  10.4 us
  transfers between devices with their start and end apart: 18, of which 18 were waited for; matrix products, arithmetic and copies ran while one was open for 2% of the time, Pallas kernels for 0%

commit v1 on v0

--- a/solution.py
+++ b/solution.py
@@ -45,7 +45,10 @@
 
     def advance_cross(step_index, loop_state):
         column_pair, factor_pair, stay_gram, moving_gram = loop_state
-        cross_term = lax.psum(gram_of(column_pair[:block_width], column_pair[block_width:]), "rows")
+        cross_term = jnp.sum(
+            lax.all_gather(gram_of(column_pair[:block_width], column_pair[block_width:]), "rows"),
+            axis=0,
+        )
         upper_half = jnp.concatenate([stay_gram, cross_term], 1)
         lower_half = jnp.concatenate([cross_term.T, moving_gram], 1)
         pair_gram = jnp.concatenate([upper_half, lower_half], 0)

time: 403 us -> 382 us (0.948)
  blocking collectives: 57.1 us -> 37.9 us
    psum x6 -> x0, blocking collectives: 46.7 us -> none  [advance_cross(): lax.psum(gram_of(column_pair[:block_width], column_pair[block_width:]), '...]
    all_gather x0 -> x6, blocking collectives: none -> 27.5 us  [advance_cross(): lax.all_gather(gram_of(column_pair[:block_width], column_pair[block_width...]
where the time goes in v1:
time: 382 us; the launch traced here: 381 us
  other arithmetic  275 us (72%)
  waiting for transfers between devices  42.7 us (11%)
  blocking collectives  37.9 us (10%)
  matrix products  17.8 us (5%)
  local copies, waits for them, and re-layouts  3.9 us (1%)
    another operation x36, other arithmetic, orth_factor(): jnp.linalg.cholesky(jnp.dot(square.T, square, precision=HIGHEST_PREC))  149 us
    another operation x24, other arithmetic, orth_factor(): jax.scipy.linalg.solve_triangular(lower_factor, square.T, lower=True)  126 us
    ppermute x18, waiting for transfers between devices, shifted(): return lax.ppermute(block, axis, route)  42.7 us
    all_gather x6, blocking collectives, advance_cross(): lax.all_gather(gram_of(column_pair[:block_width], column_pair[block_width...  27.5 us
    psum x1, blocking collectives, body(): lax.psum((gram_of(columns[:block_width], columns[:block_width]), gram_of(...  10.4 us
  transfers between devices with their start and end apart: 18, of which 18 were waited for; matrix products, arithmetic and copies ran while one was open for 2% of the time, Pallas kernels for 0%

profile of v1, /device:TPU:0, one launch (start us, length us, event | category | flops | bytes accessed | tf_op | source)
XLA Modules:
  0.0 381.5 jit_solution(16539425070175047870)
XLA Ops:
  2.2 10.4 %all-reduce = (f32[64,64]{1,0:T(8,128)S(1)}, f32[64,64]{1,0:T(8,128)S(1)}) all-reduce(f32[64,64]{1,0:T(8,128)S(1)} %fusion.17, f32[64,64]{1,0:T(8,128)S(1)} %fusion.15), channel_id=1, replica_groups=mesh['blk'=16,'rows'=2] {'rows'}, use_global_device_ids=true, to_apply=%region_0.0 | all-reduce | flops 8192 | bytes 65536 | tf_op jit(solution)/shard_map/psum | solution.py:38
  12.7 368.1 %while.16 = (s32[]{:T(128)}, f32[128,640]{1,0:T(8,128)S(1)}, f32[128,256]{1,0:T(8,128)S(1)}, f32[64,64]{1,0:T(8,128)S(1)}, f32[64,64]{1,0:T(8,128)S(1)}, /*index=5*/s32[]{:T(128)}, f32[]{:T(128)}) while((s32[]{:T(128)}, f32[128,640]{1,0:T(8,128)S(1)}, f32[128,256]{1,0:T(8,128)S(1)}, f32[64,64]{1,0:T(8,128)S(1)}, f32[64,64]{1,0:T(8,128)S(1)}, ...), condition=%wide.region_6.9_spmd, body=%wide.region_2.8_spmd.sunk | while | flops 384241920 | bytes 6834381 | solution.py:77
  13.0 4.6 %all-gather.2 = f32[128,64]{1,0:T(8,128)S(1)} all-gather(f32[64,64]{1,0:T(8,128)S(1)} %fusion.101), channel_id=2, replica_groups=mesh['blk'=16,'rows'=2] {'rows'}, dimensions={0}, use_global_device_ids=true | all-gather | bytes 49152 | tf_op jit(solution)/shard_map/while/body/eval_jaxpr/all_gather | solution.py:49
  18.2 11.7 %cholesky.144 = f32[128,128]{1,0:T(8,128)S(1)} custom-call(f32[128,128]{1,0:T(8,128)S(1)} %fusion.103), custom_call_target="Cholesky" | custom-call | tf_op jit(solution)/shard_map/while/body/eval_jaxpr/jit(cholesky)/cholesky | solution.py:17
  31.2 9.8 %custom-call.10 = f32[1,128,128]{1,2,0:T(8,128)S(1)} custom-call(f32[1,128,128]{2,1,0:T(8,128)S(1)} %fusion.105), custom_call_target="InvertDiagBlocksLowerTriangular" | custom-call | tf_op jit(solution)/shard_map/while/body/eval_jaxpr/jit(_solve_triangular)/triangular_solve | solution.py:18
  42.0 11.7 %cholesky.145 = f32[128,128]{1,0:T(8,128)S(1)} custom-call(f32[128,128]{1,0:T(8,128)S(1)} %fusion.109), custom_call_target="Cholesky" | custom-call | tf_op jit(solution)/shard_map/while/body/eval_jaxpr/jit(cholesky)/cholesky | solution.py:17
  55.1 9.8 %custom-call.11 = f32[1,128,128]{1,2,0:T(8,128)S(1)} custom-call(f32[1,128,128]{2,1,0:T(8,128)S(1)} %fusion.110), custom_call_target="InvertDiagBlocksLowerTriangular" | custom-call | tf_op jit(solution)/shard_map/while/body/eval_jaxpr/jit(_solve_triangular)/triangular_solve | solution.py:18
  79.6 11.7 %cholesky.144 = f32[128,128]{1,0:T(8,128)S(1)} custom-call(f32[128,128]{1,0:T(8,128)S(1)} %fusion.103), custom_call_target="Cholesky" | custom-call | tf_op jit(solution)/shard_map/while/body/eval_jaxpr/jit(cholesky)/cholesky | solution.py:17
  92.7 9.8 %custom-call.10 = f32[1,128,128]{1,2,0:T(8,128)S(1)} custom-call(f32[1,128,128]{2,1,0:T(8,128)S(1)} %fusion.105), custom_call_target="InvertDiagBlocksLowerTriangular" | custom-call | tf_op jit(solution)/shard_map/while/body/eval_jaxpr/jit(_solve_triangular)/triangular_solve | solution.py:18
  103.4 11.7 %cholesky.145 = f32[128,128]{1,0:T(8,128)S(1)} custom-call(f32[128,128]{1,0:T(8,128)S(1)} %fusion.109), custom_call_target="Cholesky" | custom-call | tf_op jit(solution)/shard_map/while/body/eval_jaxpr/jit(cholesky)/cholesky | solution.py:17
  116.5 9.8 %custom-call.11 = f32[1,128,128]{1,2,0:T(8,128)S(1)} custom-call(f32[1,128,128]{2,1,0:T(8,128)S(1)} %fusion.110), custom_call_target="InvertDiagBlocksLowerTriangular" | custom-call | tf_op jit(solution)/shard_map/while/body/eval_jaxpr/jit(_solve_triangular)/triangular_solve | solution.py:18
  128.1 5.3 %collective-permute-done.1 = f32[64,256]{1,0:T(8,128)S(1)} collective-permute-done((f32[64,256]{1,0:T(8,128)S(1)}, f32[64,256]{1,0:T(8,128)S(1)}, u32[]{:S(2)}, u32[]{:S(2)}) %collective-permute-start.1) | collective-permute-done | bytes 65568 | tf_op jit(solution)/shard_map/while/body/eval_jaxpr/ppermute | solution.py:13
  140.9 11.7 %cholesky.144 = f32[128,128]{1,0:T(8,128)S(1)} custom-call(f32[128,128]{1,0:T(8,128)S(1)} %fusion.103), custom_call_target="Cholesky" | custom-call | tf_op jit(solution)/shard_map/while/body/eval_jaxpr/jit(cholesky)/cholesky | solution.py:17
  154.0 9.8 %custom-call.10 = f32[1,128,128]{1,2,0:T(8,128)S(1)} custom-call(f32[1,128,128]{2,1,0:T(8,128)S(1)} %fusion.105), custom_call_target="InvertDiagBlocksLowerTriangular" | custom-call | tf_op jit(solution)/shard_map/while/body/eval_jaxpr/jit(_solve_triangular)/triangular_solve | solution.py:18
  164.8 11.7 %cholesky.145 = f32[128,128]{1,0:T(8,128)S(1)} custom-call(f32[128,128]{1,0:T(8,128)S(1)} %fusion.109), custom_call_target="Cholesky" | custom-call | tf_op jit(solution)/shard_map/while/body/eval_jaxpr/jit(cholesky)/cholesky | solution.py:17
  177.8 9.8 %custom-call.11 = f32[1,128,128]{1,2,0:T(8,128)S(1)} custom-call(f32[1,128,128]{2,1,0:T(8,128)S(1)} %fusion.110), custom_call_target="InvertDiagBlocksLowerTriangular" | custom-call | tf_op jit(solution)/shard_map/while/body/eval_jaxpr/jit(_solve_triangular)/triangular_solve | solution.py:18
  189.4 5.3 %collective-permute-done.1 = f32[64,256]{1,0:T(8,128)S(1)} collective-permute-done((f32[64,256]{1,0:T(8,128)S(1)}, f32[64,256]{1,0:T(8,128)S(1)}, u32[]{:S(2)}, u32[]{:S(2)}) %collective-permute-start.1) | collective-permute-done | bytes 65568 | tf_op jit(solution)/shard_map/while/body/eval_jaxpr/ppermute | solution.py:13
  202.3 11.7 %cholesky.144 = f32[128,128]{1,0:T(8,128)S(1)} custom-call(f32[128,128]{1,0:T(8,128)S(1)} %fusion.103), custom_call_target="Cholesky" | custom-call | tf_op jit(solution)/shard_map/while/body/eval_jaxpr/jit(cholesky)/cholesky | solution.py:17
  215.3 9.8 %custom-call.10 = f32[1,128,128]{1,2,0:T(8,128)S(1)} custom-call(f32[1,128,128]{2,1,0:T(8,128)S(1)} %fusion.105), custom_call_target="InvertDiagBlocksLowerTriangular" | custom-call | tf_op jit(solution)/shard_map/while/body/eval_jaxpr/jit(_solve_triangular)/triangular_solve | solution.py:18
  226.1 11.7 %cholesky.145 = f32[128,128]{1,0:T(8,128)S(1)} custom-call(f32[128,128]{1,0:T(8,128)S(1)} %fusion.109), custom_call_target="Cholesky" | custom-call | tf_op jit(solution)/shard_map/while/body/eval_jaxpr/jit(cholesky)/cholesky | solution.py:17
  239.1 9.8 %custom-call.11 = f32[1,128,128]{1,2,0:T(8,128)S(1)} custom-call(f32[1,128,128]{2,1,0:T(8,128)S(1)} %fusion.110), custom_call_target="InvertDiagBlocksLowerTriangular" | custom-call | tf_op jit(solution)/shard_map/while/body/eval_jaxpr/jit(_solve_triangular)/triangular_solve | solution.py:18
  250.7 5.3 %collective-permute-done.1 = f32[64,256]{1,0:T(8,128)S(1)} collective-permute-done((f32[64,256]{1,0:T(8,128)S(1)}, f32[64,256]{1,0:T(8,128)S(1)}, u32[]{:S(2)}, u32[]{:S(2)}) %collective-permute-start.1) | collective-permute-done | bytes 65568 | tf_op jit(solution)/shard_map/while/body/eval_jaxpr/ppermute | solution.py:13
  263.6 11.7 %cholesky.144 = f32[128,128]{1,0:T(8,128)S(1)} custom-call(f32[128,128]{1,0:T(8,128)S(1)} %fusion.103), custom_call_target="Cholesky" | custom-call | tf_op jit(solution)/shard_map/while/body/eval_jaxpr/jit(cholesky)/cholesky | solution.py:17
  276.6 9.8 %custom-call.10 = f32[1,128,128]{1,2,0:T(8,128)S(1)} custom-call(f32[1,128,128]{2,1,0:T(8,128)S(1)} %fusion.105), custom_call_target="InvertDiagBlocksLowerTriangular" | custom-call | tf_op jit(solution)/shard_map/while/body/eval_jaxpr/jit(_solve_triangular)/triangular_solve | solution.py:18
  287.4 11.7 %cholesky.145 = f32[128,128]{1,0:T(8,128)S(1)} custom-call(f32[128,128]{1,0:T(8,128)S(1)} %fusion.109), custom_call_target="Cholesky" | custom-call | tf_op jit(solution)/shard_map/while/body/eval_jaxpr/jit(cholesky)/cholesky | solution.py:17
  300.5 9.8 %custom-call.11 = f32[1,128,128]{1,2,0:T(8,128)S(1)} custom-call(f32[1,128,128]{2,1,0:T(8,128)S(1)} %fusion.110), custom_call_target="InvertDiagBlocksLowerTriangular" | custom-call | tf_op jit(solution)/shard_map/while/body/eval_jaxpr/jit(_solve_triangular)/triangular_solve | solution.py:18
  312.0 5.3 %collective-permute-done.1 = f32[64,256]{1,0:T(8,128)S(1)} collective-permute-done((f32[64,256]{1,0:T(8,128)S(1)}, f32[64,256]{1,0:T(8,128)S(1)}, u32[]{:S(2)}, u32[]{:S(2)}) %collective-permute-start.1) | collective-permute-done | bytes 65568 | tf_op jit(solution)/shard_map/while/body/eval_jaxpr/ppermute | solution.py:13
  324.9 11.7 %cholesky.144 = f32[128,128]{1,0:T(8,128)S(1)} custom-call(f32[128,128]{1,0:T(8,128)S(1)} %fusion.103), custom_call_target="Cholesky" | custom-call | tf_op jit(solution)/shard_map/while/body/eval_jaxpr/jit(cholesky)/cholesky | solution.py:17
  338.0 9.8 %custom-call.10 = f32[1,128,128]{1,2,0:T(8,128)S(1)} custom-call(f32[1,128,128]{2,1,0:T(8,128)S(1)} %fusion.105), custom_call_target="InvertDiagBlocksLowerTriangular" | custom-call | tf_op jit(solution)/shard_map/while/body/eval_jaxpr/jit(_solve_triangular)/triangular_solve | solution.py:18
  348.7 11.7 %cholesky.145 = f32[128,128]{1,0:T(8,128)S(1)} custom-call(f32[128,128]{1,0:T(8,128)S(1)} %fusion.109), custom_call_target="Cholesky" | custom-call | tf_op jit(solution)/shard_map/while/body/eval_jaxpr/jit(cholesky)/cholesky | solution.py:17
  361.8 9.8 %custom-call.11 = f32[1,128,128]{1,2,0:T(8,128)S(1)} custom-call(f32[1,128,128]{2,1,0:T(8,128)S(1)} %fusion.110), custom_call_target="InvertDiagBlocksLowerTriangular" | custom-call | tf_op jit(solution)/shard_map/while/body/eval_jaxpr/jit(_solve_triangular)/triangular_solve | solution.py:18
  373.3 5.3 %collective-permute-done.1 = f32[64,256]{1,0:T(8,128)S(1)} collective-permute-done((f32[64,256]{1,0:T(8,128)S(1)}, f32[64,256]{1,0:T(8,128)S(1)}, u32[]{:S(2)}, u32[]{:S(2)}) %collective-permute-start.1) | collective-permute-done | bytes 65568 | tf_op jit(solution)/shard_map/while/body/eval_jaxpr/ppermute | solution.py:13
  (213 shorter events, 80.1 us)
Async XLA Ops:
  1.9 10.8 %copy-start.2 = (f32[128,256]{1,0:T(8,128)S(1)}, f32[128,256]{1,0:T(8,128)}, u32[]{:S(2)}) copy-start(f32[128,256]{1,0:T(8,128)} %param.8) | copy-start | bytes 393220
  65.5 6.4 %collective-permute-start.1 = (f32[64,256]{1,0:T(8,128)S(1)}, f32[64,256]{1,0:T(8,128)S(1)}, u32[]{:S(2)}, u32[]{:S(2)}) collective-permute-start(f32[64,256]{1,0:T(8,128)S(1)} %get-tuple-element.91), channel_id=1, source_target_pairs={{30,0},{0,2},{2,4},{4,6},{6,8},{8,10},{10,12},{12,14},{14,16},{16,... | collective-permute-start | bytes 196616 | tf_op jit(solution)/shard_map/while/body/eval_jaxpr/ppermute | solution.py:13
  66.0 7.7 %collective-permute-start = (f32[64,640]{1,0:T(8,128)S(1)}, f32[64,640]{1,0:T(8,128)S(1)}, u32[]{:S(2)}, u32[]{:S(2)}) collective-permute-start(f32[64,640]{1,0:T(8,128)S(1)} %get-tuple-element.89), channel_id=1, source_target_pairs={{30,0},{0,2},{2,4},{4,6},{6,8},{8,10},{10,12},{12,14},{14,16},{16,... | collective-permute-start | bytes 491528 | tf_op jit(solution)/shard_map/while/body/eval_jaxpr/ppermute | solution.py:13
  68.1 6.0 %collective-permute-start.2 = (f32[64,64]{1,0:T(8,128)S(1)}, f32[64,64]{1,0:T(8,128)S(1)}, u32[]{:S(2)}, u32[]{:S(2)}) collective-permute-start(f32[64,64]{1,0:T(8,128)S(1)} %get-tuple-element.94), channel_id=1, source_target_pairs={{30,0},{0,2},{2,4},{4,6},{6,8},{8,10},{10,12},{12,14},{14,16},{16,... | collective-permute-start | bytes 49160 | tf_op jit(solution)/shard_map/while/body/eval_jaxpr/ppermute | solution.py:13
  126.9 6.4 %collective-permute-start.1 = (f32[64,256]{1,0:T(8,128)S(1)}, f32[64,256]{1,0:T(8,128)S(1)}, u32[]{:S(2)}, u32[]{:S(2)}) collective-permute-start(f32[64,256]{1,0:T(8,128)S(1)} %get-tuple-element.91), channel_id=1, source_target_pairs={{30,0},{0,2},{2,4},{4,6},{6,8},{8,10},{10,12},{12,14},{14,16},{16,... | collective-permute-start | bytes 196616 | tf_op jit(solution)/shard_map/while/body/eval_jaxpr/ppermute | solution.py:13
  127.4 7.7 %collective-permute-start = (f32[64,640]{1,0:T(8,128)S(1)}, f32[64,640]{1,0:T(8,128)S(1)}, u32[]{:S(2)}, u32[]{:S(2)}) collective-permute-start(f32[64,640]{1,0:T(8,128)S(1)} %get-tuple-element.89), channel_id=1, source_target_pairs={{30,0},{0,2},{2,4},{4,6},{6,8},{8,10},{10,12},{12,14},{14,16},{16,... | collective-permute-start | bytes 491528 | tf_op jit(solution)/shard_map/while/body/eval_jaxpr/ppermute | solution.py:13
  128.0 7.4 %collective-permute-start.2 = (f32[64,64]{1,0:T(8,128)S(1)}, f32[64,64]{1,0:T(8,128)S(1)}, u32[]{:S(2)}, u32[]{:S(2)}) collective-permute-start(f32[64,64]{1,0:T(8,128)S(1)} %get-tuple-element.94), channel_id=1, source_target_pairs={{30,0},{0,2},{2,4},{4,6},{6,8},{8,10},{10,12},{12,14},{14,16},{16,... | collective-permute-start | bytes 49160 | tf_op jit(solution)/shard_map/while/body/eval_jaxpr/ppermute | solution.py:13
  188.2 6.4 %collective-permute-start.1 = (f32[64,256]{1,0:T(8,128)S(1)}, f32[64,256]{1,0:T(8,128)S(1)}, u32[]{:S(2)}, u32[]{:S(2)}) collective-permute-start(f32[64,256]{1,0:T(8,128)S(1)} %get-tuple-element.91), channel_id=1, source_target_pairs={{30,0},{0,2},{2,4},{4,6},{6,8},{8,10},{10,12},{12,14},{14,16},{16,... | collective-permute-start | bytes 196616 | tf_op jit(solution)/shard_map/while/body/eval_jaxpr/ppermute | solution.py:13
  188.7 7.7 %collective-permute-start = (f32[64,640]{1,0:T(8,128)S(1)}, f32[64,640]{1,0:T(8,128)S(1)}, u32[]{:S(2)}, u32[]{:S(2)}) collective-permute-start(f32[64,640]{1,0:T(8,128)S(1)} %get-tuple-element.89), channel_id=1, source_target_pairs={{30,0},{0,2},{2,4},{4,6},{6,8},{8,10},{10,12},{12,14},{14,16},{16,... | collective-permute-start | bytes 491528 | tf_op jit(solution)/shard_map/while/body/eval_jaxpr/ppermute | solution.py:13
  189.4 7.4 %collective-permute-start.2 = (f32[64,64]{1,0:T(8,128)S(1)}, f32[64,64]{1,0:T(8,128)S(1)}, u32[]{:S(2)}, u32[]{:S(2)}) collective-permute-start(f32[64,64]{1,0:T(8,128)S(1)} %get-tuple-element.94), channel_id=1, source_target_pairs={{30,0},{0,2},{2,4},{4,6},{6,8},{8,10},{10,12},{12,14},{14,16},{16,... | collective-permute-start | bytes 49160 | tf_op jit(solution)/shard_map/while/body/eval_jaxpr/ppermute | solution.py:13
  249.5 6.4 %collective-permute-start.1 = (f32[64,256]{1,0:T(8,128)S(1)}, f32[64,256]{1,0:T(8,128)S(1)}, u32[]{:S(2)}, u32[]{:S(2)}) collective-permute-start(f32[64,256]{1,0:T(8,128)S(1)} %get-tuple-element.91), channel_id=1, source_target_pairs={{30,0},{0,2},{2,4},{4,6},{6,8},{8,10},{10,12},{12,14},{14,16},{16,... | collective-permute-start | bytes 196616 | tf_op jit(solution)/shard_map/while/body/eval_jaxpr/ppermute | solution.py:13
  250.1 7.7 %collective-permute-start = (f32[64,640]{1,0:T(8,128)S(1)}, f32[64,640]{1,0:T(8,128)S(1)}, u32[]{:S(2)}, u32[]{:S(2)}) collective-permute-start(f32[64,640]{1,0:T(8,128)S(1)} %get-tuple-element.89), channel_id=1, source_target_pairs={{30,0},{0,2},{2,4},{4,6},{6,8},{8,10},{10,12},{12,14},{14,16},{16,... | collective-permute-start | bytes 491528 | tf_op jit(solution)/shard_map/while/body/eval_jaxpr/ppermute | solution.py:13
  250.7 7.4 %collective-permute-start.2 = (f32[64,64]{1,0:T(8,128)S(1)}, f32[64,64]{1,0:T(8,128)S(1)}, u32[]{:S(2)}, u32[]{:S(2)}) collective-permute-start(f32[64,64]{1,0:T(8,128)S(1)} %get-tuple-element.94), channel_id=1, source_target_pairs={{30,0},{0,2},{2,4},{4,6},{6,8},{8,10},{10,12},{12,14},{14,16},{16,... | collective-permute-start | bytes 49160 | tf_op jit(solution)/shard_map/while/body/eval_jaxpr/ppermute | solution.py:13
  310.9 6.4 %collective-permute-start.1 = (f32[64,256]{1,0:T(8,128)S(1)}, f32[64,256]{1,0:T(8,128)S(1)}, u32[]{:S(2)}, u32[]{:S(2)}) collective-permute-start(f32[64,256]{1,0:T(8,128)S(1)} %get-tuple-element.91), channel_id=1, source_target_pairs={{30,0},{0,2},{2,4},{4,6},{6,8},{8,10},{10,12},{12,14},{14,16},{16,... | collective-permute-start | bytes 196616 | tf_op jit(solution)/shard_map/while/body/eval_jaxpr/ppermute | solution.py:13
  311.4 7.7 %collective-permute-start = (f32[64,640]{1,0:T(8,128)S(1)}, f32[64,640]{1,0:T(8,128)S(1)}, u32[]{:S(2)}, u32[]{:S(2)}) collective-permute-start(f32[64,640]{1,0:T(8,128)S(1)} %get-tuple-element.89), channel_id=1, source_target_pairs={{30,0},{0,2},{2,4},{4,6},{6,8},{8,10},{10,12},{12,14},{14,16},{16,... | collective-permute-start | bytes 491528 | tf_op jit(solution)/shard_map/while/body/eval_jaxpr/ppermute | solution.py:13
  312.0 7.4 %collective-permute-start.2 = (f32[64,64]{1,0:T(8,128)S(1)}, f32[64,64]{1,0:T(8,128)S(1)}, u32[]{:S(2)}, u32[]{:S(2)}) collective-permute-start(f32[64,64]{1,0:T(8,128)S(1)} %get-tuple-element.94), channel_id=1, source_target_pairs={{30,0},{0,2},{2,4},{4,6},{6,8},{8,10},{10,12},{12,14},{14,16},{16,... | collective-permute-start | bytes 49160 | tf_op jit(solution)/shard_map/while/body/eval_jaxpr/ppermute | solution.py:13
  372.2 6.4 %collective-permute-start.1 = (f32[64,256]{1,0:T(8,128)S(1)}, f32[64,256]{1,0:T(8,128)S(1)}, u32[]{:S(2)}, u32[]{:S(2)}) collective-permute-start(f32[64,256]{1,0:T(8,128)S(1)} %get-tuple-element.91), channel_id=1, source_target_pairs={{30,0},{0,2},{2,4},{4,6},{6,8},{8,10},{10,12},{12,14},{14,16},{16,... | collective-permute-start | bytes 196616 | tf_op jit(solution)/shard_map/while/body/eval_jaxpr/ppermute | solution.py:13
  372.7 7.7 %collective-permute-start = (f32[64,640]{1,0:T(8,128)S(1)}, f32[64,640]{1,0:T(8,128)S(1)}, u32[]{:S(2)}, u32[]{:S(2)}) collective-permute-start(f32[64,640]{1,0:T(8,128)S(1)} %get-tuple-element.89), channel_id=1, source_target_pairs={{30,0},{0,2},{2,4},{4,6},{6,8},{8,10},{10,12},{12,14},{14,16},{16,... | collective-permute-start | bytes 491528 | tf_op jit(solution)/shard_map/while/body/eval_jaxpr/ppermute | solution.py:13
  373.3 7.4 %collective-permute-start.2 = (f32[64,64]{1,0:T(8,128)S(1)}, f32[64,64]{1,0:T(8,128)S(1)}, u32[]{:S(2)}, u32[]{:S(2)}) collective-permute-start(f32[64,64]{1,0:T(8,128)S(1)} %get-tuple-element.94), channel_id=1, source_target_pairs={{30,0},{0,2},{2,4},{4,6},{6,8},{8,10},{10,12},{12,14},{14,16},{16,... | collective-permute-start | bytes 49160 | tf_op jit(solution)/shard_map/while/body/eval_jaxpr/ppermute | solution.py:13
  380.7 0.7 copy-start
  380.7 0.8 copy-start.1
